TPU v7x, 512 devices: a whole 4x8x8 slice. The times are simulated.
512 devices in a mesh: elem: 128 (over z, y, core), gpt: 4 (over x).
Axes of the slice: x: 4, y: 8, z: 8, core: 2. Of those that a mesh axis runs over, the one named last changes fastest.
Arguments:
- slab_kelvin: float32 [16, 65536], P(None, 'elem'), may hold values from 190 to 310
- moisture_mass_load: float32 [16, 65536], P(None, 'elem'), may hold values from 0.1 to 1
- dioxide_mass_load: float32 [16, 65536], P(None, 'elem'), may hold values from 0.2 to 1
- slab_depth_share: float32 [16, 65536], P(None, 'elem'), may hold values from 0.01 to 0.06
- lower_node_slot: int32 [16, 65536], P(None, 'elem'), may hold values from 0 to 57
- upper_node_share: float32 [16, 65536], P(None, 'elem'), may hold values from 0 to 1
- ground_skin_kelvin: float32 [65536], P('elem'), may hold values from 230 to 310
- ground_reflectivity: float32 [65536], P('elem'), may hold values from 0.05 to 0.8
- sun_angle_class: int32 [65536], P('elem'), may hold values from 0 to 127, as said below
- owner_profile_routes: int32 [65536], P('elem'), may hold values from 0 to 511, as said below
- sunlit_angle_factors: float32 [64], replicated, may hold values from 0.05 to 1
- thermal_absorptivity: bfloat16 [128, 118], P('gpt'), may hold values from 0.0019989014 to 2
- sunlight_absorptivity: bfloat16 [112, 118], P('gpt'), may hold values from 0.0019989014 to 1
- emission_quadrature_share: float32 [128], P('gpt'), may hold values from 0.00390625 to 0.015625
- insolation_quadrature_share: float32 [112], P('gpt'), may hold values from 0.004464286 to 0.017857144
Outputs:
- heat_lw: float32 [16, 65536], P('gpt', 'elem')
- heat_sw: float32 [16, 65536], P('gpt', 'elem')
- surface_flux: float32 [4, 65536], P('gpt', 'elem')
Inputs may be any that keep to these rules, and one draw needn't show every extreme that they name: `sun_angle_class`: A column is sunlit when its bin is below 64. Every span receives exactly 256 sunlit columns, and an owner gives equally many sunlit columns to every span. `owner_profile_routes`: for each owner, a permutation of its local column numbers 0 to 511.
All inputs are finite; a program needn't handle non-finite values.
Results may differ from a plain program's by a relative error of at most 0.0014.
Values may be sent and summed in bfloat16 or wider, within the bound.
A program may use at most 64 MiB of HBM per device.

v0:
```python
import jax
import jax.numpy as jnp
from jax import lax
from jax.sharding import PartitionSpec as P


def in_blocks(array, dim, count):
    dims = array.shape
    parts = array.reshape(*dims[:dim], count, dims[dim] // count, *dims[dim + 1 :])
    return jnp.moveaxis(parts, dim, 0)


def summed_on_arrival(array, axis, dim):
    parts = in_blocks(array, dim, lax.axis_size(axis))
    arrived = lax.all_to_all(parts, axis, split_axis=0, concat_axis=0, tiled=True)
    return arrived.sum(axis=0)


def zenith_cosine(bins, table):
    node_index = jnp.arange(table.shape[0], dtype=jnp.int32)[:, None]
    return jnp.sum(jnp.where(bins[None, :] == node_index, table[:, None], 0.0), axis=0)


def absorber(state_inputs, node_count):
    node_values = jnp.arange(node_count).astype(state_inputs.dtype)[:, None, None]
    node_index = state_inputs[4][None]
    weight = state_inputs[5][None]
    interp_weights = jnp.where(node_values == node_index, 1.0 - weight, 0.0) + jnp.where(
        node_values == node_index + 1.0, weight, 0.0
    )
    amount = jnp.concatenate(
        [interp_weights * state_inputs[1][None], interp_weights * state_inputs[2][None]], axis=0
    ).astype(jnp.bfloat16)
    return amount.reshape(2 * node_count, -1)


def longwave(tau, state_inputs, profile, planck):
    layered = jnp.moveaxis(tau, 1, 0)
    warmth = (state_inputs[0] / 250.0) ** 4

    def sweep_step(carry, inputs):
        depth, heat = inputs
        transmit = jnp.exp(-1.66 * depth)
        emitted = planck[:, None] * heat[None] * (1.0 - transmit)
        carry = transmit * carry + emitted
        return (carry, jnp.sum(carry, axis=0))

    ground = planck[:, None] * (profile[0][None] / 250.0) ** 4
    _, down_sums = lax.scan(sweep_step, jnp.zeros_like(ground), (layered, warmth))
    _, up_sums = lax.scan(sweep_step, ground, (layered, warmth), reverse=True)
    down_faces = jnp.concatenate([jnp.zeros_like(down_sums[:1]), down_sums], axis=0)
    up_faces = jnp.concatenate([up_sums, jnp.sum(ground, axis=0)[None]], axis=0)
    net_faces = up_faces - down_faces
    heating = (net_faces[1:] - net_faces[:-1]) / state_inputs[3]
    return (heating, down_sums[-1], up_sums[0])


def shortwave(tau, state_inputs, profile, solar):
    layered = jnp.moveaxis(tau, 1, 0)
    sun_height_factor = profile[2]
    safe_cosine = jnp.where(sun_height_factor > 0.0, sun_height_factor, 1.0)
    incident = solar[:, None] * sun_height_factor[None]

    def beam_step(carry, depth):
        carry = carry * jnp.exp(-depth / safe_cosine[None])
        return (carry, jnp.sum(carry, axis=0))

    beam_last, direct_sums = lax.scan(beam_step, incident, layered)
    ground = profile[1][None] * beam_last

    def rise_step(carry, depth):
        carry = carry * jnp.exp(-1.66 * depth)
        return (carry, jnp.sum(carry, axis=0))

    _, reflected_sums = lax.scan(rise_step, ground, layered, reverse=True)
    direct_faces = jnp.concatenate([jnp.sum(incident, axis=0)[None], direct_sums], axis=0)
    reflected_faces = jnp.concatenate([reflected_sums, jnp.sum(ground, axis=0)[None]], axis=0)
    net_faces = direct_faces - reflected_faces
    heating = (net_faces[:-1] - net_faces[1:]) / state_inputs[3]
    return (heating, direct_sums[-1], reflected_sums[0])


def radiate(state_inputs, profile, thermal_absorptivity, sunlight_absorptivity, planck, solar):
    node_count = thermal_absorptivity.shape[1] // 2
    slab_heights = state_inputs.shape[1]
    profile_ordinal = state_inputs.shape[2]
    amount = absorber(state_inputs, node_count)
    tau_long = jnp.dot(thermal_absorptivity, amount, preferred_element_type=jnp.float32).reshape(
        thermal_absorptivity.shape[0], slab_heights, profile_ordinal
    )
    heat_long, down_ground, outgoing = longwave(tau_long, state_inputs, profile, planck)
    tau_short = jnp.dot(sunlight_absorptivity, amount, preferred_element_type=jnp.float32).reshape(
        sunlight_absorptivity.shape[0], slab_heights, profile_ordinal
    )
    heat_short, direct_ground, reflected = shortwave(tau_short, state_inputs, profile, solar)
    return (
        jnp.stack([heat_long, heat_short], axis=1),
        jnp.stack([down_ground, outgoing, direct_ground, reflected], axis=0),
    )


def blockwise(work, state_inputs, profile):
    profile_ordinal = state_inputs.shape[2]
    block_size = min(profile_ordinal, 256)
    block_total = profile_ordinal // block_size

    def one_block(block_start):
        field_part = lax.dynamic_slice_in_dim(state_inputs, block_start, block_size, 2)
        side_part = lax.dynamic_slice_in_dim(profile, block_start, block_size, 1)
        return work(field_part, side_part)

    heating, fluxes = lax.map(one_block, jnp.arange(block_total, dtype=jnp.int32) * block_size)
    heating = jnp.moveaxis(heating, 0, 2).reshape(heating.shape[1], 2, profile_ordinal)
    fluxes = jnp.moveaxis(fluxes, 0, 1).reshape(4, profile_ordinal)
    return (heating, fluxes)


def local(
    slab_kelvin,
    moisture_mass_load,
    dioxide_mass_load,
    slab_depth_share,
    lower_node_slot,
    upper_node_share,
    ground_skin_kelvin,
    ground_reflectivity,
    sun_angle_class,
    owner_profile_routes,
    sunlit_angle_factors,
    thermal_absorptivity,
    sunlight_absorptivity,
    emission_quadrature_share,
    insolation_quadrature_share,
):
    slab_heights, profile_ordinal = slab_kelvin.shape
    group_size = lax.axis_size("gpt")
    sun_height_factor = zenith_cosine(sun_angle_class, sunlit_angle_factors)
    state_inputs = jnp.stack(
        [
            slab_kelvin,
            moisture_mass_load,
            dioxide_mass_load,
            slab_depth_share,
            lower_node_slot.astype(jnp.float32),
            upper_node_share,
        ]
    )
    profile = jnp.stack([ground_skin_kelvin, ground_reflectivity, sun_height_factor])
    pieces = (state_inputs, profile, True)
    long_table, short_table, planck_all, solar_all = (
        thermal_absorptivity,
        sunlight_absorptivity,
        emission_quadrature_share,
        insolation_quadrature_share,
    )
    field_piece, side_piece, sunny = pieces

    def work(field_part, side_part, sunny=sunny):
        return radiate(field_part, side_part, long_table, short_table, planck_all, solar_all)

    heat_piece, flux_piece = blockwise(work, field_piece, side_piece)
    local_count = heat_piece.shape[2]
    heat_share, flux_share = (
        summed_on_arrival(heat_piece.reshape(2 * slab_heights, local_count), "gpt", 0),
        summed_on_arrival(flux_piece, "gpt", 0),
    )
    owned = heat_share
    surface_flux = lax.all_to_all(
        flux_share[:, owner_profile_routes], "elem", split_axis=1, concat_axis=1, tiled=True
    )
    owned = owned.reshape(slab_heights // group_size, 2, profile_ordinal)
    return (owned[:, 0], owned[:, 1], surface_flux)


def solution(mesh):
    in_specs = (
        P(None, "elem"),
        P(None, "elem"),
        P(None, "elem"),
        P(None, "elem"),
        P(None, "elem"),
        P(None, "elem"),
        P("elem"),
        P("elem"),
        P("elem"),
        P("elem"),
        P(),
        P("gpt", None),
        P("gpt", None),
        P("gpt"),
        P("gpt"),
    )
    out_specs = (P("gpt", "elem"), P("gpt", "elem"), P("gpt", "elem"))
    return jax.shard_map(local, mesh=mesh, in_specs=in_specs, out_specs=out_specs, check_vma=False)
```

profile of v0, /device:TPU:1, one launch (start us, length us, event | category | flops | bytes accessed | tf_op | source)
XLA Modules:
  0.0 89.7 jit_solution(664948712098474023)
XLA Ops:
  0.7 0.8 bitcast_dynamic-update-slice_fusion.5
  1.4 0.8 bitcast_dynamic-update-slice_fusion.4
  2.2 0.8 bitcast_dynamic-update-slice_fusion.3
  2.9 0.8 bitcast_dynamic-update-slice_fusion.2
  3.7 0.8 bitcast_dynamic-update-slice_fusion.1
  4.5 0.8 bitcast_dynamic-update-slice_fusion
  5.2 0.8 select_reduce_fusion
  6.7 30.2 %while.153 = (s32[]{:T(128)}, f32[2,16,2,256]{3,1,2,0:T(8,128)S(1)}, f32[2,4,256]{2,1,0:T(4,128)S(1)}, f32[32]{0:T(128)}, s32[2]{0:T(128)S(1)}, /*index=5*/f32[3...) while((s32[]{:T(128)}, f32[2,16,2,256]{3,1,2,0:T(8,128)S(1)}, ...), condition=%wide.region_17.18_spmd, body=%wide.region_1.17_spmd.sunk | while | flops 64328532 | bytes 9267961 | solution.py:112
  11.5 1.6 %while.156 = (s32[]{:T(128)}, f32[28,256]{1,0:T(8,128)S(1)}, f32[16,256]{1,0:T(8,128)S(1)}, f32[16,28,256]{2,1,0:T(8,128)S(1)}, f32[256]{0:T(256)S(1)}, /*index=5*/s32[]{:T(128)}, s32[]{:T(128)}) while((s32[]{:T(128)}, f32[28,256]{1,0:T(8,128)S(1)}, f32[16,256]{1,0:T(8,128)S(1)}, f32[16,28,256]{2,1,0:T(8,128)S(1)}, f32[256]{0:T(256)S(1)}, ...), condition=%wide.region_12.12_spmd, body=%wide.region_10.11_spmd.sunk | while | flops 28418 | bytes 90197 | solution.py:68
  13.2 1.6 %while.157 = (s32[]{:T(128)}, f32[28,256]{1,0:T(8,128)S(1)}, f32[16,256]{1,0:T(8,128)S(1)}, f32[16,28,256]{2,1,0:T(8,128)S(1)}, s32[]{:T(128)}, /*index=5*/s32[]{:T(128)}, s32[]{:T(128)}) while((s32[]{:T(128)}, f32[28,256]{1,0:T(8,128)S(1)}, f32[16,256]{1,0:T(8,128)S(1)}, f32[16,28,256]{2,1,0:T(8,128)S(1)}, s32[]{:T(128)}, ...), condition=%wide.region_15.15_spmd, body=%wide.region_13.14_spmd.sunk | while | flops 21251 | bytes 89185 | solution.py:75
  15.8 2.7 %while.155 = (s32[]{:T(128)}, f32[32,256]{1,0:T(8,128)S(1)}, f32[16,256]{1,0:T(8,128)S(1)}, f32[16,32,256]{2,1,0:T(8,128)S(1)}, f32[32]{0:T(128)S(1)}, /*index=5*/f32[16,256]{1,0:T(8,128)S(1)}, s32[]{:T(128)}, s32[]{:T(128)}) while((s32[]{:T(128)}, f32[32,256]{1,0:T(8,128)S(1)}, f32[16,256]{1,0:T(8,128)S(1)}, ...), condition=%wide.region_8.8_spmd.clone, body=%wide.region_6.7_spmd.clone.sunk | while | flops 65283 | bytes 104683 | solution.py:49
  18.6 2.7 %while.154 = (s32[]{:T(128)}, f32[32,256]{1,0:T(8,128)S(1)}, f32[16,256]{1,0:T(8,128)S(1)}, f32[16,32,256]{2,1,0:T(8,128)S(1)}, f32[32]{0:T(128)S(1)}, /*index=5...) while((s32[]{:T(128)}, f32[32,256]{1,0:T(8,128)S(1)}, f32[16,256]{1,0:T(8,128)S(1)}, ...), condition=%wide.region_4.4_spmd, body=%wide.region_2.3_spmd.sunk | while | flops 57091 | bytes 104693 | solution.py:50
  26.6 1.6 %while.156 = (s32[]{:T(128)}, f32[28,256]{1,0:T(8,128)S(1)}, f32[16,256]{1,0:T(8,128)S(1)}, f32[16,28,256]{2,1,0:T(8,128)S(1)}, f32[256]{0:T(256)S(1)}, /*index=5*/s32[]{:T(128)}, s32[]{:T(128)}) while((s32[]{:T(128)}, f32[28,256]{1,0:T(8,128)S(1)}, f32[16,256]{1,0:T(8,128)S(1)}, f32[16,28,256]{2,1,0:T(8,128)S(1)}, f32[256]{0:T(256)S(1)}, ...), condition=%wide.region_12.12_spmd, body=%wide.region_10.11_spmd.sunk | while | flops 28418 | bytes 90197 | solution.py:68
  28.3 1.6 %while.157 = (s32[]{:T(128)}, f32[28,256]{1,0:T(8,128)S(1)}, f32[16,256]{1,0:T(8,128)S(1)}, f32[16,28,256]{2,1,0:T(8,128)S(1)}, s32[]{:T(128)}, /*index=5*/s32[]{:T(128)}, s32[]{:T(128)}) while((s32[]{:T(128)}, f32[28,256]{1,0:T(8,128)S(1)}, f32[16,256]{1,0:T(8,128)S(1)}, f32[16,28,256]{2,1,0:T(8,128)S(1)}, s32[]{:T(128)}, ...), condition=%wide.region_15.15_spmd, body=%wide.region_13.14_spmd.sunk | while | flops 21251 | bytes 89185 | solution.py:75
  30.9 2.7 %while.155 = (s32[]{:T(128)}, f32[32,256]{1,0:T(8,128)S(1)}, f32[16,256]{1,0:T(8,128)S(1)}, f32[16,32,256]{2,1,0:T(8,128)S(1)}, f32[32]{0:T(128)S(1)}, /*index=5*/f32[16,256]{1,0:T(8,128)S(1)}, s32[]{:T(128)}, s32[]{:T(128)}) while((s32[]{:T(128)}, f32[32,256]{1,0:T(8,128)S(1)}, f32[16,256]{1,0:T(8,128)S(1)}, ...), condition=%wide.region_8.8_spmd.clone, body=%wide.region_6.7_spmd.clone.sunk | while | flops 65283 | bytes 104683 | solution.py:49
  33.7 2.7 %while.154 = (s32[]{:T(128)}, f32[32,256]{1,0:T(8,128)S(1)}, f32[16,256]{1,0:T(8,128)S(1)}, f32[16,32,256]{2,1,0:T(8,128)S(1)}, f32[32]{0:T(128)S(1)}, /*index=5...) while((s32[]{:T(128)}, f32[32,256]{1,0:T(8,128)S(1)}, f32[16,256]{1,0:T(8,128)S(1)}, ...), condition=%wide.region_4.4_spmd, body=%wide.region_2.3_spmd.sunk | while | flops 57091 | bytes 104693 | solution.py:50
  37.6 4.8 %all-to-all-start.1 = ((f32[4,1,512]{2,1,0:T(1,128)}), f32[4,1,512]{2,1,0:T(1,128)S(1)}, u32[]{:S(2)}, u32[]{:S(2)}) async-start(f32[4,1,512]{2,1,0:T(1,128)} %copy.31), calls=%async_computation.1 | async-start | bytes 16384 | tf_op jit(solution)/shard_map/all_to_all | solution.py:15
  42.5 4.1 %all-to-all-done.1 = f32[4,1,512]{2,1,0:T(1,128)S(1)} async-done(((f32[4,1,512]{2,1,0:T(1,128)}), f32[4,1,512]{2,1,0:T(1,128)S(1)}, u32[]{:S(2)}, u32[]{:S(2)}) %all-to-all-start.1) | async-done | bytes 8224 | tf_op jit(solution)/shard_map/all_to_all | solution.py:15
  46.6 3.5 %gather_fusion = f32[512]{0:T(512)S(1)} fusion(f32[512]{0:T(512)S(1)} %reduce_sum.123, s32[1024]{0:T(1024)S(1)} %pad_clamp_fusion), kind=kCustom, calls=%fused_computation | custom fusion | bytes 6144 | tf_op jit(solution)/shard_map/gather | solution.py:169
  50.8 19.0 %all-to-all-start.2 = ((f32[1,128,4]{2,0,1:T(1,128)}), f32[1,128,4]{2,0,1:T(1,128)S(1)}, u32[]{:S(2)}, u32[]{:S(2)}) async-start(f32[1,128,4]{2,0,1:T(1,128)} %bitcast.36), calls=%async_computation.2 | async-start | bytes 131072 | tf_op jit(solution)/shard_map/all_to_all | solution.py:168
  70.6 10.7 %all-to-all-done.2 = f32[1,128,4]{2,0,1:T(1,128)S(1)} async-done(((f32[1,128,4]{2,0,1:T(1,128)}), f32[1,128,4]{2,0,1:T(1,128)S(1)}, u32[]{:S(2)}, u32[]{:S(2)}) %all-to-all-start.2) | async-done | bytes 2080 | tf_op jit(solution)/shard_map/all_to_all | solution.py:168
  81.3 3.3 %all-to-all-start = ((f32[4,8,512]{2,1,0:T(8,128)}), f32[4,8,512]{2,1,0:T(8,128)S(1)}, u32[]{:S(2)}, u32[]{:S(2)}) async-start(f32[4,8,512]{2,1,0:T(8,128)} %reshape_reshape_reshape.3), calls=%async_computation | async-start | bytes 131072 | tf_op jit(solution)/shard_map/all_to_all | solution.py:15
  85.1 0.8 reduce.4
  86.6 2.4 %all-to-all-done = f32[4,8,512]{2,1,0:T(8,128)S(1)} async-done(((f32[4,8,512]{2,1,0:T(8,128)}), f32[4,8,512]{2,1,0:T(8,128)S(1)}, u32[]{:S(2)}, u32[]{:S(2)}) %all-to-all-start) | async-done | bytes 65568 | tf_op jit(solution)/shard_map/all_to_all | solution.py:15
  (427 shorter events, 27.2 us)
Async XLA Ops:
  6.7 35.7 %copy-start.3 = (s32[512]{0:T(512)S(1)}, s32[512]{0:T(512)}, u32[]{:S(2)}) copy-start(s32[512]{0:T(512)} %param.34) | copy-start | bytes 6148
  9.5 0.7 copy-start.5
  10.7 0.7 copy-start.2
  13.1 1.7 %copy-start.4 = (bf16[32,118]{1,0:T(8,128)(2,1)S(1)}, bf16[32,118]{1,0:T(8,128)(2,1)}, u32[]{:S(2)}) copy-start(bf16[32,118]{1,0:T(8,128)(2,1)} %get-tuple-element.1083) | copy-start | bytes 22660 | tf_op jit(solution)/shard_map/while
  15.1 0.7 copy-start
  21.4 0.5 copy-start.1
  24.6 0.7 copy-start.5
  25.8 0.7 copy-start.2
  28.2 1.7 %copy-start.4 = (bf16[32,118]{1,0:T(8,128)(2,1)S(1)}, bf16[32,118]{1,0:T(8,128)(2,1)}, u32[]{:S(2)}) copy-start(bf16[32,118]{1,0:T(8,128)(2,1)} %get-tuple-element.1083) | copy-start | bytes 22660 | tf_op jit(solution)/shard_map/while
  30.2 0.7 copy-start
  36.5 0.5 copy-start.1
  37.6 9.0 %all-to-all-start.1 = ((f32[4,1,512]{2,1,0:T(1,128)}), f32[4,1,512]{2,1,0:T(1,128)S(1)}, u32[]{:S(2)}, u32[]{:S(2)}) async-start(f32[4,1,512]{2,1,0:T(1,128)} %copy.31), calls=%async_computation.1 | async-start | bytes 16384 | tf_op jit(solution)/shard_map/all_to_all | solution.py:15
  50.8 30.5 %all-to-all-start.2 = ((f32[1,128,4]{2,0,1:T(1,128)}), f32[1,128,4]{2,0,1:T(1,128)S(1)}, u32[]{:S(2)}, u32[]{:S(2)}) async-start(f32[1,128,4]{2,0,1:T(1,128)} %bitcast.36), calls=%async_computation.2 | async-start | bytes 131072 | tf_op jit(solution)/shard_map/all_to_all | solution.py:168
  81.3 7.7 %all-to-all-start = ((f32[4,8,512]{2,1,0:T(8,128)}), f32[4,8,512]{2,1,0:T(8,128)S(1)}, u32[]{:S(2)}, u32[]{:S(2)}) async-start(f32[4,8,512]{2,1,0:T(8,128)} %reshape_reshape_reshape.3), calls=%async_computation | async-start | bytes 131072 | tf_op jit(solution)/shard_map/all_to_all | solution.py:15
where the time goes:
time: 90.7 us; the launch traced here: 89.7 us
  starting transfers between devices  27.1 us (30%)
  local copies, waits for them, and re-layouts  22.2 us (24%)
  waiting for transfers between devices  17.3 us (19%)
  other arithmetic  13.5 us (15%)
  loops' own time  7.74 us (9%)
  matrix products  1.12 us (1%)
    all_to_all x1, starting transfers between devices, local(): lax.all_to_all(flux_share[:, owner_profile_routes], 'elem', split_axis=1,...  19 us
    all_to_all x1, waiting for transfers between devices, local(): lax.all_to_all(flux_share[:, owner_profile_routes], 'elem', split_axis=1,...  10.7 us
    all_to_all x2, starting transfers between devices, summed_on_arrival(): lax.all_to_all(parts, axis, split_axis=0, concat_axis=0, tiled=True)  8.11 us
    all_to_all x2, waiting for transfers between devices, summed_on_arrival(): lax.all_to_all(parts, axis, split_axis=0, concat_axis=0, tiled=True)  6.57 us
    reduce_sum x64, other arithmetic, sweep_step(): return (carry, jnp.sum(carry, axis=0))  5.99 us
    dynamic_update_slice x128, local copies, waits for them, and re-layouts, longwave(): lax.scan(sweep_step, jnp.zeros_like(ground), (layered, warmth))  4.95 us
    another operation x1, loops' own time, blockwise(): lax.map(one_block, jnp.arange(block_total, dtype=jnp.int32) * block_size)  4.43 us
    unnamed x7, local copies, waits for them, and re-layouts  3.66 us
  transfers between devices with their start and end apart: 3, of which 3 were waited for; matrix products, arithmetic and copies ran while one was open for 2% of the time, Pallas kernels for 0%

commit v1 on v0

v1 whole, which is shorter than its diff:
```python
import jax
import jax.numpy as jnp
from jax import lax
from jax.experimental import pallas as pl
from jax.experimental.pallas import tpu as pltpu
from jax.sharding import PartitionSpec as P

MESH = pl.DeviceIdType.MESH
LOG2E = 1.4426950408889634
DIFFUSE = -1.66 * LOG2E
LAYERS = 16
COLS = 512
LANES = 128
WIDE = 256
NODES = 59
GL = 32
GS = 28
GPT = 4
NZ = 8
NW = 16
STACK = 10


def by_lane(row, index):
    return jnp.take_along_axis(row, index, axis=1, mode="promise_in_bounds")


def as_column(row, length):
    r = lax.broadcasted_iota(jnp.int32, (length, length), 0)
    c = lax.broadcasted_iota(jnp.int32, (length, length), 1)
    return jnp.sum(jnp.where(r == c, jnp.broadcast_to(row, (length, length)), 0.0), axis=1, keepdims=True)


def kernel(
    kelvin, moisture, dioxide, depth, slot, share, skin, albedo, bins, routes, table,
    thermal, sunlight, planck, solar,
    heat_lw, heat_sw, flux_out,
    coef, rows, cosine, trans, emit, down_sum, direct_sum, up_sum, reflect_sum, flux, heat, heat_in,
    part, part_in, mine, z_in, w_out, w_in,
    heat_send, heat_recv, part_send, part_recv, z_send, z_recv, w_send, w_recv,
):
    e = lax.axis_index("elem")
    q = lax.axis_index("gpt")
    z = e // NW
    w = e % NW
    barrier = pltpu.get_barrier_semaphore()

    def gpt_peer(i):
        return {"elem": e, "gpt": (q + i) % GPT}

    def z_peer(i):
        return {"elem": ((z + i) % NZ) * NW + w, "gpt": q}

    def w_peer(i):
        return {"elem": z * NW + (w + i) % NW, "gpt": q}

    for i in range(1, GPT):
        pl.semaphore_signal(barrier, inc=1, device_id=gpt_peer(i), device_id_type=MESH)
    for i in range(1, NZ):
        pl.semaphore_signal(barrier, inc=1, device_id=z_peer(i), device_id_type=MESH)
    for i in range(1, NW):
        pl.semaphore_signal(barrier, inc=1, device_id=w_peer(i), device_id_type=MESH)

    coef[...] = jnp.zeros_like(coef)
    coef[0:GL, 0 : 2 * NODES] = thermal[...]
    coef[GL : GL + GS, 0 : 2 * NODES] = sunlight[...]
    rows[...] = lax.broadcasted_iota(jnp.int32, (LANES, WIDE), 0).astype(jnp.float32).astype(jnp.bfloat16)
    p_col = as_column(planck[...], GL)
    s_col = as_column(solar[...], GS)
    s_col = jnp.concatenate([s_col, jnp.zeros((GL - GS, 1), jnp.float32)], axis=0)

    factors = jnp.concatenate([table[...], table[...]], axis=1)
    factors = jnp.broadcast_to(factors, (8, LANES))
    for k in range(COLS // LANES):
        b = bins[:, k * LANES : (k + 1) * LANES]
        picked = by_lane(factors, jnp.broadcast_to(b & 63, (8, LANES)))[0:1]
        cosine[:, k * LANES : (k + 1) * LANES] = jnp.where(b < 64, picked, 0.0)

    a = coef[...]
    for half in range(COLS // WIDE):
        cols = pl.ds(half * WIDE, WIDE)
        cos = cosine[:, cols]
        slant = -LOG2E / jnp.where(cos > 0.0, cos, 1.0)

        def down_step(l, carry):
            down, direct = carry
            at = pl.ds(l, 1)
            upper = share[at, cols]
            lower = 1.0 - upper
            m = moisture[at, cols]
            d = dioxide[at, cols]
            node = slot[at, cols].astype(jnp.float32)
            bf = jnp.bfloat16
            n0 = node.astype(bf)
            n1 = (node + 1.0).astype(bf)
            n2 = (node + NODES).astype(bf)
            n3 = (node + (NODES + 1)).astype(bf)
            m0 = (lower * m).astype(bf)
            m1 = (upper * m).astype(bf)
            d0 = (lower * d).astype(bf)
            d1 = (upper * d).astype(bf)
            zero = jnp.zeros((), bf)
            r = rows[0:48, :]
            top = jnp.where(r == n0, m0, jnp.where(r == n1, m1, zero))
            r = rows[48:64, :]
            mid = jnp.where(r == n0, m0, jnp.where(r == n1, m1, jnp.where(r == n2, d0, jnp.where(r == n3, d1, zero))))
            r = rows[64:128, :]
            low = jnp.where(r == n2, d0, jnp.where(r == n3, d1, zero))
            amount = jnp.concatenate([top, mid, low], axis=0)
            tau = jnp.dot(a, amount, preferred_element_type=jnp.float32)
            tau_lw = tau[0:GL]
            tau_sw = tau[GL : 2 * GL]
            x = kelvin[at, cols] * (1.0 / 250.0)
            x = x * x
            warm = x * x
            t = jnp.exp2(tau_lw * DIFFUSE)
            source = (p_col * warm) * (1.0 - t)
            down = t * down + source
            trans[l, 0:GL, :] = t
            emit[l] = source
            down_sum[at, cols] = jnp.sum(down, axis=0, keepdims=True)
            trans[l, GL : 2 * GL, :] = jnp.exp2(tau_sw * DIFFUSE)
            direct = direct * jnp.exp2(tau_sw * slant)
            direct_sum[at, cols] = jnp.sum(direct, axis=0, keepdims=True)
            return down, direct

        incident = s_col * cos
        down, direct = lax.fori_loop(0, LAYERS, down_step, (jnp.zeros((GL, WIDE), jnp.float32), incident))

        x = skin[:, cols] * (1.0 / 250.0)
        x = x * x
        up = p_col * (x * x)
        reflected = albedo[:, cols] * direct

        def up_step(k, carry):
            up, reflected = carry
            l = LAYERS - 1 - k
            up = trans[l, 0:GL, :] * up + emit[l]
            up_sum[pl.ds(l, 1), cols] = jnp.sum(up, axis=0, keepdims=True)
            reflected = reflected * trans[l, GL : 2 * GL, :]
            reflect_sum[pl.ds(l, 1), cols] = jnp.sum(reflected, axis=0, keepdims=True)
            return up, reflected

        up_sum[LAYERS : LAYERS + 1, cols] = jnp.sum(up, axis=0, keepdims=True)
        reflect_sum[LAYERS : LAYERS + 1, cols] = jnp.sum(reflected, axis=0, keepdims=True)
        up, reflected = lax.fori_loop(0, LAYERS, up_step, (up, reflected))
        first = jnp.sum(incident, axis=0, keepdims=True)
        flux[0:1, cols] = down_sum[LAYERS - 1 : LAYERS, cols]
        flux[1:2, cols] = up_sum[0:1, cols]
        flux[2:3, cols] = direct_sum[LAYERS - 1 : LAYERS, cols]
        flux[3:4, cols] = reflect_sum[0:1, cols]
        for l in range(LAYERS):
            inverse = 1.0 / depth[l : l + 1, cols]
            low_net = up_sum[l + 1 : l + 2, cols] - down_sum[l : l + 1, cols]
            if l:
                top_net = up_sum[l : l + 1, cols] - down_sum[l - 1 : l, cols]
                top_sun = direct_sum[l - 1 : l, cols] - reflect_sum[l : l + 1, cols]
            else:
                top_net = up_sum[0:1, cols]
                top_sun = first - reflect_sum[0:1, cols]
            low_sun = direct_sum[l : l + 1, cols] - reflect_sum[l + 1 : l + 2, cols]
            heat[l // 4, l % 4 : l % 4 + 1, cols] = (low_net - top_net) * inverse
            heat[l // 4, 4 + l % 4 : 5 + l % 4, cols] = (top_sun - low_sun) * inverse

    order = routes[...]
    for k in range(COLS // LANES):
        index = jnp.broadcast_to(order[:, k * LANES : (k + 1) * LANES], (8, LANES))
        within = index & (LANES - 1)
        block = index >> 7
        picked = jnp.zeros((8, LANES), jnp.float32)
        for s in range(COLS // LANES):
            picked = jnp.where(block == s, by_lane(flux[:, s * LANES : (s + 1) * LANES], within), picked)
        for r in range(4):
            part[r, k : k + 1, :] = picked[r : r + 1]

    pl.semaphore_wait(barrier, (GPT - 1) + (NZ - 1) + (NW - 1))

    part_copies = []
    for i in range(1, GPT):
        c = pltpu.make_async_remote_copy(
            src_ref=part.at[(q + i) % GPT], dst_ref=part_in.at[i - 1],
            send_sem=part_send.at[i - 1], recv_sem=part_recv.at[i - 1],
            device_id=gpt_peer(i), device_id_type=MESH,
        )
        c.start()
        part_copies.append(c)
    heat_copies = []
    for i in range(1, GPT):
        c = pltpu.make_async_remote_copy(
            src_ref=heat.at[(q + i) % GPT], dst_ref=heat_in.at[i - 1],
            send_sem=heat_send.at[i - 1], recv_sem=heat_recv.at[i - 1],
            device_id=gpt_peer(i), device_id_type=MESH,
        )
        c.start()
        heat_copies.append(c)
    for c in part_copies:
        c.wait_recv()
    whole = part[q] + part_in[0] + part_in[1] + part_in[2]
    for k in range(4):
        mine[k] = whole[k : k + 1]

    z_copies = []
    for i in range(1, NZ):
        to = (z + i) % NZ
        c = pltpu.make_async_remote_copy(
            src_ref=mine.at[to // 2], dst_ref=z_in.at[z],
            send_sem=z_send.at[i - 1], recv_sem=z_recv.at[i - 1],
            device_id=z_peer(i), device_id_type=MESH,
        )
        c.start()
        z_copies.append(c)
    z_in[z] = mine[z // 2]

    for c in heat_copies:
        c.wait_recv()
    owned = heat[q] + heat_in[0] + heat_in[1] + heat_in[2]
    heat_lw[...] = owned[0:4]
    heat_sw[...] = owned[4:8]

    for c in z_copies:
        c.wait_recv()
    half_start = 16 * (z % 2)
    lane = lax.broadcasted_iota(jnp.int32, (NW, LANES), 1) >> 2
    line = lax.broadcasted_iota(jnp.int32, (NW, LANES), 0)
    source = (lane + (32 - half_start) - line) & 31
    out = jnp.zeros((NW, LANES), jnp.float32)
    for s in range(NZ):
        row = z_in[s]
        if s:
            row = pltpu.roll(row, 4 * s, 1)
        out = jnp.where(source == s, jnp.broadcast_to(row, (NW, LANES)), out)
    for k in range(NW):
        w_out[k] = out[k : k + 1]

    w_copies = []
    for i in range(1, NW):
        c = pltpu.make_async_remote_copy(
            src_ref=w_out.at[(w + i) % NW], dst_ref=w_in.at[w],
            send_sem=w_send.at[i - 1], recv_sem=w_recv.at[i - 1],
            device_id=w_peer(i), device_id_type=MESH,
        )
        c.start()
        w_copies.append(c)
    w_in[w] = w_out[w]
    for c in w_copies:
        c.wait_recv()
    start = half_start + w
    lane = lax.broadcasted_iota(jnp.int32, (NZ, LANES), 1) >> 2
    line = lax.broadcasted_iota(jnp.int32, (NZ, LANES), 0)
    source = (lane + (32 - start) - line) & 31
    out = jnp.zeros((NZ, LANES), jnp.float32)
    for s in range(NW):
        row = w_in[s]
        if s:
            row = pltpu.roll(row, 4 * s, 1)
        out = jnp.where(source == s, jnp.broadcast_to(row, (NZ, LANES)), out)
    out = pltpu.roll(out, (LANES - 4 * start) % LANES, 1)
    first_half = lax.broadcasted_iota(jnp.int32, (1, LANES), 1) < 64
    for k in range(4):
        even = pltpu.roll(out, (LANES - 8 * k) % LANES, 1) if k else out
        odd = pltpu.roll(out, (LANES - 4 * (2 * k + 1) + 64) % LANES, 1)
        flux_out[:, k * LANES : (k + 1) * LANES] = jnp.where(
            first_half, even[2 * k : 2 * k + 1], odd[2 * k + 1 : 2 * k + 2]
        )

    for c in part_copies + heat_copies + z_copies + w_copies:
        c.wait_send()


def local(
    slab_kelvin, moisture_mass_load, dioxide_mass_load, slab_depth_share, lower_node_slot, upper_node_share,
    ground_skin_kelvin, ground_reflectivity, sun_angle_class, owner_profile_routes, sunlit_angle_factors,
    thermal_absorptivity, sunlight_absorptivity, emission_quadrature_share, insolation_quadrature_share,
):
    f32 = jnp.float32
    vmem = pl.BlockSpec(memory_space=pltpu.VMEM)
    dma = pltpu.SemaphoreType.DMA
    return pl.pallas_call(
        kernel,
        out_shape=(
            jax.ShapeDtypeStruct((LAYERS // GPT, COLS), f32),
            jax.ShapeDtypeStruct((LAYERS // GPT, COLS), f32),
            jax.ShapeDtypeStruct((1, COLS), f32),
        ),
        in_specs=[vmem] * 15,
        out_specs=(vmem, vmem, vmem),
        scratch_shapes=[
            pltpu.VMEM((2 * GL, LANES), jnp.bfloat16),
            pltpu.VMEM((LANES, WIDE), jnp.bfloat16),
            pltpu.VMEM((1, COLS), f32),
            pltpu.VMEM((LAYERS, 2 * GL, WIDE), f32),
            pltpu.VMEM((LAYERS, GL, WIDE), f32),
            pltpu.VMEM((LAYERS, COLS), f32),
            pltpu.VMEM((LAYERS, COLS), f32),
            pltpu.VMEM((24, COLS), f32),
            pltpu.VMEM((24, COLS), f32),
            pltpu.VMEM((8, COLS), f32),
            pltpu.VMEM((GPT, 8, COLS), f32),
            pltpu.VMEM((GPT - 1, 8, COLS), f32),
            pltpu.VMEM((GPT, 4, LANES), f32),
            pltpu.VMEM((GPT - 1, 4, LANES), f32),
            pltpu.VMEM((4, 1, LANES), f32),
            pltpu.VMEM((NZ, 1, LANES), f32),
            pltpu.VMEM((NW, 1, LANES), f32),
            pltpu.VMEM((NW, 1, LANES), f32),
            dma((GPT - 1,)), dma((GPT - 1,)), dma((GPT - 1,)), dma((GPT - 1,)),
            dma((NZ - 1,)), dma((NZ - 1,)), dma((NW - 1,)), dma((NW - 1,)),
        ],
        compiler_params=pltpu.CompilerParams(collective_id=0, has_side_effects=True),
    )(
        slab_kelvin, moisture_mass_load, dioxide_mass_load, slab_depth_share, lower_node_slot, upper_node_share,
        ground_skin_kelvin.reshape(1, COLS), ground_reflectivity.reshape(1, COLS),
        sun_angle_class.reshape(1, COLS), owner_profile_routes.reshape(1, COLS),
        sunlit_angle_factors.reshape(1, 64), thermal_absorptivity, sunlight_absorptivity,
        emission_quadrature_share.reshape(1, GL), insolation_quadrature_share.reshape(1, GS),
    )


def solution(mesh):
    e = P("elem")
    eg = P(None, "elem")
    in_specs = (eg,) * 6 + (e,) * 4 + (P(), P("gpt", None), P("gpt", None), P("gpt"), P("gpt"))
    out_specs = (P("gpt", "elem"), P("gpt", "elem"), P("gpt", "elem"))
    return jax.shard_map(local, mesh=mesh, in_specs=in_specs, out_specs=out_specs, check_vma=False)
```

time: 90.7 us -> 37 us (0.41)
  Pallas kernels: 0 us -> 33.5 us
  starting transfers between devices: 27.1 us -> 0 us
  local copies, waits for them, and re-layouts: 22.2 us -> 2.55 us
  waiting for transfers between devices: 17.3 us -> 0 us
  other arithmetic: 13.5 us -> 0 us
  loops' own time: 7.74 us -> 0 us
  matrix products: 1.12 us -> 0 us
    pallas_call x0 -> x1, Pallas kernels: none -> 33.5 us  [local(): pl.pallas_call(kernel, out_shape=(jax.ShapeDtypeStruct((LAYERS // GPT, CO...]
    all_to_all x3 -> x0, starting transfers between devices: 27.1 us -> none  [the longest x1 19 us: local(): lax.all_to_all(flux_share[:, owner_profile_routes], 'elem', split_axis=1,...]
    all_to_all x3 -> x0, waiting for transfers between devices: 17.3 us -> none  [the longest x1 10.7 us: local(): lax.all_to_all(flux_share[:, owner_profile_routes], 'elem', split_axis=1,...]
    reduce_sum x135 -> x0, other arithmetic: 9.67 us -> none  [the longest x64 5.99 us: sweep_step(): return (carry, jnp.sum(carry, axis=0))]
    another operation x9 -> x0, loops' own time: 7.74 us -> none  [the longest x1 4.43 us: blockwise(): lax.map(one_block, jnp.arange(block_total, dtype=jnp.int32) * block_size)]
    dynamic_update_slice x128 -> x0, local copies, waits for them, and re-layouts: 4.95 us -> none  [longwave(): lax.scan(sweep_step, jnp.zeros_like(ground), (layered, warmth))]
    while x34 -> x0, local copies, waits for them, and re-layouts: 3.55 us -> none
    gather x1 -> x0, local copies, waits for them, and re-layouts: 3.49 us -> none  [local(): flux_share[:, owner_profile_routes]]
  transfers between devices with their start and end apart: 3 -> 0, of which waited for: 3 -> 0; matrix products, arithmetic and copies ran while one was open for 2% -> 0% of each run, Pallas kernels for 0% -> 0%
where the time goes in v1:
time: 37 us; the launch traced here: 36.7 us
  Pallas kernels  33.5 us (91%)
  local copies, waits for them, and re-layouts  2.55 us (7%)
  between operations  0.66 us (2%)
    pallas_call x1, Pallas kernels, local(): pl.pallas_call(kernel, out_shape=(jax.ShapeDtypeStruct((LAYERS // GPT, CO...  33.5 us
    unnamed x7, local copies, waits for them, and re-layouts  2.55 us

profile of v1, /device:TPU:1, one launch (start us, length us, event | category | flops | bytes accessed | tf_op | source)
XLA Modules:
  0.0 36.7 jit_solution(18416721118255277148)
XLA Ops:
  0.6 33.5 %shard_map.166 = (f32[4,512]{1,0:T(4,128)}, f32[4,512]{1,0:T(4,128)}, f32[1,512]{1,0:T(1,128)}) custom-call(f32[16,512]{1,0:T(8,128)} %kelvin.1, f32[16,512]{1,0:T(8,128)} %moisture.1, f32[16,512]{1,0:T(8,128)} %dioxide.1, f32[16,512]{1,0:T(8,128)} %depth.1, s32[16,512]{1,0:T(8,128)} %slot.1, f32[16,512]{1,0:T(8,128)} %share.1, f32[1,512]{1,0:T(1,128)} %bitcast.7, ...), custom_call_target="tpu_custom_call" | custom-call | tf_op jit(solution)/shard_map/pallas_call | solution.py:278
  34.2 0.0 copy-start
  34.2 1.3 %copy.21 = f32[4,512]{1,0:T(4,128)} copy(f32[4,512]{1,0:T(4,128)} %get-tuple-element.6) | data formatting | bytes 16384
  35.5 0.0 copy-done
  35.5 0.0 copy-start.1
  35.5 0.6 %copy.22 = f32[4,512]{1,0:T(4,128)} copy(f32[4,512]{1,0:T(4,128)S(1)} %copy-done) | data formatting | bytes 16384
  36.1 0.1 copy-done.1
  36.1 0.6 %copy.23 = f32[1,512]{1,0:T(1,128)} copy(f32[1,512]{1,0:T(1,128)S(1)} %copy-done.1) | data formatting | bytes 4096
Async XLA Ops:
  34.2 1.3 %copy-start = (f32[4,512]{1,0:T(4,128)S(1)}, f32[4,512]{1,0:T(4,128)}, u32[]{:S(2)}) copy-start(f32[4,512]{1,0:T(4,128)} %get-tuple-element.7) | copy-start | bytes 24580
  35.5 0.7 %copy-start.1 = (f32[1,512]{1,0:T(1,128)S(1)}, f32[1,512]{1,0:T(1,128)}, u32[]{:S(2)}) copy-start(f32[1,512]{1,0:T(1,128)} %get-tuple-element.8) | copy-start | bytes 6148

commit v2 on v1

v2 whole, which is shorter than its diff:
```python
import jax
import jax.numpy as jnp
from jax import lax
from jax.experimental import pallas as pl
from jax.experimental.pallas import tpu as pltpu
from jax.sharding import PartitionSpec as P

MESH = pl.DeviceIdType.MESH
LOG2E = 1.4426950408889634
DIFFUSE = -1.66 * LOG2E
LAYERS = 16
COLS = 512
LANES = 128
WIDE = 256
NODES = 59
GL = 32
GS = 28
GPT = 4
NZ = 8
NW = 16
UNROLL = 4
HEAT_UNROLL = 2
F32 = jnp.float32
BF16 = jnp.bfloat16

ZQ_STEPS = sorted(
    [(dz, dq) for dz in range(NZ) for dq in range(GPT) if dz or dq],
    key=lambda s: -(min(s[0], NZ - s[0]) + min(s[1], GPT - s[1])),
)
W_STEPS = sorted(range(1, NW), key=lambda s: -min(s, NW - s))


def by_lane(row, index):
    return jnp.take_along_axis(row, index, axis=1, mode="promise_in_bounds")


def as_column(row, length):
    r = lax.broadcasted_iota(jnp.int32, (length, length), 0)
    c = lax.broadcasted_iota(jnp.int32, (length, length), 1)
    return jnp.sum(jnp.where(r == c, jnp.broadcast_to(row, (length, length)), 0.0), axis=1, keepdims=True)


def total(x):
    return jnp.sum(x, axis=0, keepdims=True)


def fourth(x):
    x = x * (1.0 / 250.0)
    x = x * x
    return x * x


def kernel(*refs):
    args, refs = refs[:15], refs[15:]
    heat_lw, heat_sw, flux_out = refs[:3]
    local, refs = refs[3:18], refs[18:]
    (
        kelvin, moisture, dioxide, depth, slot, share, skin, albedo, bins, routes, table,
        thermal, sunlight, planck, solar,
    ) = local
    (
        coef, rows, cosine, node, m0, m1, d0, d1, warm, trans, emit, tau_sun,
        down_sum, direct_sum, up_sum, reflect_sum, net, sun, flux, heat, heat_in,
        part, zq_in, w_out, w_in,
        load_sem, heat_send, heat_recv, zq_send, zq_recv, w_send, w_recv,
    ) = refs
    e = lax.axis_index("elem")
    q = lax.axis_index("gpt")
    z = e // NW
    w = e % NW
    barrier = pltpu.get_barrier_semaphore()

    loads = [pltpu.make_async_copy(args[i], local[i], load_sem.at[i]) for i in range(15)]
    for c in loads:
        c.start()

    def zq_peer(dz, dq):
        return {"elem": ((z + dz) % NZ) * NW + w, "gpt": (q + dq) % GPT}

    def w_peer(dw):
        return {"elem": z * NW + (w + dw) % NW, "gpt": q}

    for dz, dq in ZQ_STEPS:
        pl.semaphore_signal(barrier, inc=1, device_id=zq_peer(dz, dq), device_id_type=MESH)
    for dw in W_STEPS:
        pl.semaphore_signal(barrier, inc=1, device_id=w_peer(dw), device_id_type=MESH)

    coef[...] = jnp.zeros_like(coef)
    rows[...] = lax.broadcasted_iota(jnp.int32, (LANES, WIDE), 0).astype(F32).astype(BF16)
    down_sum[0:1, :] = jnp.zeros((1, COLS), F32)
    for c in loads:
        c.wait()
    coef[0:GL, 0 : 2 * NODES] = thermal[...]
    coef[GL : GL + GS, 0 : 2 * NODES] = sunlight[...]
    p_col = as_column(planck[...], GL)
    s_col = as_column(solar[...], GS)
    s_col = jnp.concatenate([s_col, jnp.zeros((GL - GS, 1), F32)], axis=0)

    upper = share[...]
    lower = 1.0 - upper
    m = moisture[...]
    d = dioxide[...]
    m0[...] = lower * m
    m1[...] = upper * m
    d0[...] = lower * d
    d1[...] = upper * d
    node[...] = slot[...].astype(F32)
    warm[...] = fourth(kelvin[...])
    factors = jnp.concatenate([table[...], table[...]], axis=1)
    factors = jnp.broadcast_to(factors, (8, LANES))
    for k in range(COLS // LANES):
        b = bins[:, k * LANES : (k + 1) * LANES]
        picked = by_lane(factors, jnp.broadcast_to(b & 63, (8, LANES)))[0:1]
        cosine[:, k * LANES : (k + 1) * LANES] = jnp.where(b < 64, picked, 0.0)

    a = coef[...]

    def spread(ref, l, cols):
        return jnp.broadcast_to(ref[pl.ds(l, 1), cols], (16, WIDE)).astype(BF16)

    def slanted(cols):
        cos = cosine[:, cols]
        return -LOG2E / jnp.where(cos > 0.0, cos, 1.0)

    for half in range(COLS // WIDE):
        cols = pl.ds(half * WIDE, WIDE)

        def flux_layer(l, carry):
            down, clear, up, depth_sun = carry
            n0 = spread(node, l, cols)
            n1 = n0 + jnp.asarray(1, BF16)
            n2 = n0 + jnp.asarray(NODES, BF16)
            n3 = n0 + jnp.asarray(NODES + 1, BF16)
            w0, w1 = spread(m0, l, cols), spread(m1, l, cols)
            c0, c1 = spread(d0, l, cols), spread(d1, l, cols)
            zero = jnp.zeros((16, WIDE), BF16)
            blocks = []
            for k in range(8):
                r = rows[16 * k : 16 * k + 16, :]
                x = zero
                if k >= 3:
                    x = jnp.where(r == n2, c0, jnp.where(r == n3, c1, x))
                if k <= 3:
                    x = jnp.where(r == n0, w0, jnp.where(r == n1, w1, x))
                blocks.append(x)
            tau = jnp.dot(a, jnp.concatenate(blocks, axis=0), preferred_element_type=F32)
            t = jnp.exp2(tau[0:GL] * DIFFUSE)
            source = (p_col * warm[pl.ds(l, 1), cols]) * (1.0 - t)
            trans[l, :, cols] = t
            emit[l, :, cols] = source
            tau_sun[l, :, cols] = tau[GL : 2 * GL]
            up = up + clear * source
            clear = clear * t
            down = t * down + source
            return down, clear, up, depth_sun + tau[GL : 2 * GL]

        def flux_step(i, carry):
            for k in range(UNROLL):
                carry = flux_layer(i * UNROLL + k, carry)
            return carry

        blank = jnp.zeros((GL, WIDE), F32)
        carry = (blank, jnp.ones((GL, WIDE), F32), blank, blank)
        down, clear, up, depth_sun = lax.fori_loop(0, LAYERS // UNROLL, flux_step, carry)
        direct = (s_col * cosine[:, cols]) * jnp.exp2(depth_sun * slanted(cols))
        flux[0:1, cols] = total(down)
        flux[1:2, cols] = total(up + clear * (p_col * fourth(skin[:, cols])))
        flux[2:3, cols] = total(direct)
        flux[3:4, cols] = total((albedo[:, cols] * direct) * jnp.exp2(depth_sun * DIFFUSE))

    order = routes[...]
    for k in range(COLS // LANES):
        index = jnp.broadcast_to(order[:, k * LANES : (k + 1) * LANES], (8, LANES))
        within = index & (LANES - 1)
        block = index >> 7
        picked = jnp.zeros((8, LANES), F32)
        for s in range(COLS // LANES):
            picked = jnp.where(block == s, by_lane(flux[:, s * LANES : (s + 1) * LANES], within), picked)
        for r in range(GPT):
            part[r, k] = picked[r : r + 1]

    pl.semaphore_wait(barrier, len(ZQ_STEPS) + len(W_STEPS))

    zq_copies = []
    for i, (dz, dq) in enumerate(ZQ_STEPS):
        c = pltpu.make_async_remote_copy(
            src_ref=part.at[(q + dq) % GPT, ((z + dz) % NZ) // 2], dst_ref=zq_in.at[q, z],
            send_sem=zq_send.at[i], recv_sem=zq_recv.at[i],
            device_id=zq_peer(dz, dq), device_id_type=MESH,
        )
        c.start()
        zq_copies.append(c)
    zq_in[q, z] = part[q, z // 2]

    for half in range(COLS // WIDE):
        cols = pl.ds(half * WIDE, WIDE)
        slant = slanted(cols)
        incident = s_col * cosine[:, cols]
        depth_sun = tau_sun[0, :, cols]
        for l in range(1, LAYERS):
            depth_sun = depth_sun + tau_sun[l, :, cols]
        ground = albedo[:, cols] * (incident * jnp.exp2(depth_sun * slant))
        skin_up = p_col * fourth(skin[:, cols])

        def heat_layer(l, carry):
            down, up, direct, reflected = carry
            k = LAYERS - 1 - l
            down = trans[l, :, cols] * down + emit[l, :, cols]
            down_sum[pl.ds(l + 1, 1), cols] = total(down)
            up = trans[k, :, cols] * up + emit[k, :, cols]
            up_sum[pl.ds(k, 1), cols] = total(up)
            direct = direct * jnp.exp2(tau_sun[l, :, cols] * slant)
            direct_sum[pl.ds(l + 1, 1), cols] = total(direct)
            reflected = reflected * jnp.exp2(tau_sun[k, :, cols] * DIFFUSE)
            reflect_sum[pl.ds(k, 1), cols] = total(reflected)
            return down, up, direct, reflected

        def heat_step(i, carry):
            for k in range(HEAT_UNROLL):
                carry = heat_layer(i * HEAT_UNROLL + k, carry)
            return carry

        up_sum[LAYERS : LAYERS + 1, cols] = total(skin_up)
        direct_sum[0:1, cols] = total(incident)
        reflect_sum[LAYERS : LAYERS + 1, cols] = total(ground)
        carry = (jnp.zeros((GL, WIDE), F32), skin_up, incident, ground)
        lax.fori_loop(0, LAYERS // HEAT_UNROLL, heat_step, carry)

    top = slice(0, LAYERS)
    low = slice(1, LAYERS + 1)
    faces = slice(0, LAYERS + 1)
    net[faces, :] = up_sum[faces, :] - down_sum[faces, :]
    sun[faces, :] = direct_sum[faces, :] - reflect_sum[faces, :]
    inverse = 1.0 / depth[...]
    lw = (net[low, :] - net[top, :]) * inverse
    sw = (sun[top, :] - sun[low, :]) * inverse
    for r in range(GPT):
        heat[r, 0:4, :] = lw[4 * r : 4 * r + 4]
        heat[r, 4:8, :] = sw[4 * r : 4 * r + 4]

    heat_copies = []
    for i in range(1, GPT):
        c = pltpu.make_async_remote_copy(
            src_ref=heat.at[(q + i) % GPT], dst_ref=heat_in.at[i - 1],
            send_sem=heat_send.at[i - 1], recv_sem=heat_recv.at[i - 1],
            device_id=zq_peer(0, i), device_id_type=MESH,
        )
        c.start()
        heat_copies.append(c)

    for c in zq_copies:
        c.wait_recv()
    half_start = 16 * (z % 2)
    lane = lax.broadcasted_iota(jnp.int32, (NW, LANES), 1) >> 2
    line = lax.broadcasted_iota(jnp.int32, (NW, LANES), 0)
    source = (lane + (32 - half_start) - line) & 31
    out = jnp.zeros((NW, LANES), F32)
    for s in range(NZ):
        row = (zq_in[0, s] + zq_in[1, s]) + (zq_in[2, s] + zq_in[3, s])
        if s:
            row = pltpu.roll(row, 4 * s, 1)
        out = jnp.where(source == s, jnp.broadcast_to(row, (NW, LANES)), out)
    for k in range(NW):
        w_out[k] = out[k : k + 1]

    w_copies = []
    for i, dw in enumerate(W_STEPS):
        c = pltpu.make_async_remote_copy(
            src_ref=w_out.at[(w + dw) % NW], dst_ref=w_in.at[w],
            send_sem=w_send.at[i], recv_sem=w_recv.at[i],
            device_id=w_peer(dw), device_id_type=MESH,
        )
        c.start()
        w_copies.append(c)
    w_in[w] = w_out[w]

    for c in heat_copies:
        c.wait_recv()
    owned = (heat[q] + heat_in[0]) + (heat_in[1] + heat_in[2])
    heat_lw[...] = owned[0:4]
    heat_sw[...] = owned[4:8]

    for c in w_copies:
        c.wait_recv()
    start = half_start + w
    lane = lax.broadcasted_iota(jnp.int32, (NZ, LANES), 1) >> 2
    line = lax.broadcasted_iota(jnp.int32, (NZ, LANES), 0)
    source = (lane + (32 - start) - line) & 31
    out = jnp.zeros((NZ, LANES), F32)
    for s in range(NW):
        row = w_in[s]
        if s:
            row = pltpu.roll(row, 4 * s, 1)
        out = jnp.where(source == s, jnp.broadcast_to(row, (NZ, LANES)), out)
    out = pltpu.roll(out, (LANES - 4 * start) % LANES, 1)
    first_half = lax.broadcasted_iota(jnp.int32, (1, LANES), 1) < 64
    for k in range(4):
        even = pltpu.roll(out, (LANES - 8 * k) % LANES, 1) if k else out
        odd = pltpu.roll(out, (LANES - 4 * (2 * k + 1) + 64) % LANES, 1)
        flux_out[:, k * LANES : (k + 1) * LANES] = jnp.where(
            first_half, even[2 * k : 2 * k + 1], odd[2 * k + 1 : 2 * k + 2]
        )

    for c in zq_copies + heat_copies + w_copies:
        c.wait_send()


def hand_out(*refs):
    for source, target in zip(refs[:3], refs[3:]):
        target[...] = source[...]


def local(
    slab_kelvin, moisture_mass_load, dioxide_mass_load, slab_depth_share, lower_node_slot, upper_node_share,
    ground_skin_kelvin, ground_reflectivity, sun_angle_class, owner_profile_routes, sunlit_angle_factors,
    thermal_absorptivity, sunlight_absorptivity, emission_quadrature_share, insolation_quadrature_share,
):
    dma = pltpu.SemaphoreType.DMA
    vmem = pl.BlockSpec(memory_space=pltpu.VMEM)
    args = (
        slab_kelvin, moisture_mass_load, dioxide_mass_load, slab_depth_share, lower_node_slot, upper_node_share,
        ground_skin_kelvin.reshape(1, COLS), ground_reflectivity.reshape(1, COLS),
        sun_angle_class.reshape(1, COLS), owner_profile_routes.reshape(1, COLS),
        sunlit_angle_factors.reshape(1, 64), thermal_absorptivity, sunlight_absorptivity,
        emission_quadrature_share.reshape(1, GL), insolation_quadrature_share.reshape(1, GS),
    )
    state = (LAYERS, COLS)
    faces = (24, COLS)
    results = ((LAYERS // GPT, COLS), (LAYERS // GPT, COLS), (1, COLS))
    held = pl.pallas_call(
        kernel,
        out_shape=tuple(pltpu.VMEM(s, F32) for s in results),
        in_specs=[pl.BlockSpec(memory_space=pl.ANY)] * 15,
        out_specs=(vmem, vmem, vmem),
        scratch_shapes=[pltpu.VMEM(x.shape, x.dtype) for x in args]
        + [
            pltpu.VMEM((2 * GL, LANES), BF16),
            pltpu.VMEM((LANES, WIDE), BF16),
            pltpu.VMEM((1, COLS), F32),
        ]
        + [pltpu.VMEM(state, F32)] * 6
        + [pltpu.VMEM((LAYERS, GL, COLS), F32)] * 3
        + [pltpu.VMEM(faces, F32)] * 6
        + [
            pltpu.VMEM((8, COLS), F32),
            pltpu.VMEM((GPT, 8, COLS), F32),
            pltpu.VMEM((GPT - 1, 8, COLS), F32),
            pltpu.VMEM((GPT, 4, 1, LANES), F32),
            pltpu.VMEM((GPT, NZ, 1, LANES), F32),
            pltpu.VMEM((NW, 1, LANES), F32),
            pltpu.VMEM((NW, 1, LANES), F32),
            dma((15,)), dma((GPT - 1,)), dma((GPT - 1,)),
            dma((len(ZQ_STEPS),)), dma((len(ZQ_STEPS),)), dma((len(W_STEPS),)), dma((len(W_STEPS),)),
        ],
        compiler_params=pltpu.CompilerParams(collective_id=0, has_side_effects=True),
    )(*args)
    return pl.pallas_call(
        hand_out,
        out_shape=tuple(jax.ShapeDtypeStruct(s, F32) for s in results),
        in_specs=[vmem] * 3,
        out_specs=(vmem, vmem, vmem),
    )(*(pltpu.with_memory_space_constraint(h, pltpu.VMEM) for h in held))


def solution(mesh):
    e = P("elem")
    eg = P(None, "elem")
    in_specs = (eg,) * 6 + (e,) * 4 + (P(), P("gpt", None), P("gpt", None), P("gpt"), P("gpt"))
    out_specs = (P("gpt", "elem"), P("gpt", "elem"), P("gpt", "elem"))
    return jax.shard_map(local, mesh=mesh, in_specs=in_specs, out_specs=out_specs, check_vma=False)
```

time: 37 us -> 28.9 us (0.78)
  Pallas kernels: 33.5 us -> 28 us
  local copies, waits for them, and re-layouts: 2.55 us -> 0 us
    pallas_call x1 -> x2, Pallas kernels: 33.5 us -> 28 us  [the longest x1 27.4 us: local(): pl.pallas_call(kernel, out_shape=tuple((pltpu.VMEM(s, F32) for s in resul...]
    unnamed x7 -> x0, local copies, waits for them, and re-layouts: 2.55 us -> none
where the time goes in v2:
time: 28.9 us; the launch traced here: 28.7 us
  Pallas kernels  28 us (97%)
  between operations  0.64 us (2%)
    pallas_call x1, Pallas kernels, local(): pl.pallas_call(kernel, out_shape=tuple((pltpu.VMEM(s, F32) for s in resul...  27.4 us
    pallas_call x1, Pallas kernels, local(): pl.pallas_call(hand_out, out_shape=tuple((jax.ShapeDtypeStruct(s, F32) fo...  0.61 us

profile of v2, /device:TPU:1, one launch (start us, length us, event | category | flops | bytes accessed | tf_op | source)
XLA Modules:
  0.0 28.7 jit_solution(13223668404490960391)
XLA Ops:
  0.6 27.4 %shard_map.166 = (f32[4,512]{1,0:T(4,128)S(1)}, f32[4,512]{1,0:T(4,128)S(1)}, f32[1,512]{1,0:T(1,128)S(1)}) custom-call(f32[16,512]{1,0:T(8,128)} %refs_0_.1, f32[16,512]{1,0:T(8,128)} %refs_1_.1, f32[16,512]{1,0:T(8,128)} %refs_2_.1, f32[16,512]{1,0:T(8,128)} %refs_3_.1, s32[16,512]{1,0:T(8,128)} %refs_4_.1, f32[16,512]{1,0:T(8,128)} %refs_5_.1, ...), custom_call_target="tpu_custom_call" | custom-call | tf_op jit(solution)/shard_map/pallas_call | solution.py:330
  28.1 0.6 %shard_map.167 = (f32[4,512]{1,0:T(4,128)}, f32[4,512]{1,0:T(4,128)}, f32[1,512]{1,0:T(1,128)}) custom-call(f32[4,512]{1,0:T(4,128)S(1)} %get-tuple-element.6.refs_0_, f32[4,512]{1,0:T(4,128)S(1)} %get-tuple-element.7.refs_1_, f32[1,512]{1,0:T(1,128)S(1)} %get-tuple-element.8.refs_2_), custom_call_target="tpu_custom_call" | custom-call | tf_op jit(solution)/shard_map/pallas_call | solution.py:357
